TPU v7x, 32 devices: a whole 2x2x4 slice. The times are simulated.
32 devices in a mesh: row: 4 (over x, core), col: 8 (over z, y).
Axes of the slice: x: 2, y: 2, z: 4, core: 2. Of those that a mesh axis runs over, the one named last changes fastest.
Arguments:
- matrix: float32 [2048, 2048], P('row', 'col'), as said below
- start_vectors: float32 [2048, 512], P(('col', 'row')), may hold values from -6 to 6
- interval: float32 [2], replicated, as said below
Outputs:
- ortho_basis: float32 [2048, 512], P(('col', 'row'))
- projected: float32 [512, 512], replicated
- residual: float32 [2048, 512], P(('col', 'row'))
Inputs may be any that keep to these rules, and one draw needn't show every extreme that they name: matrix is exactly symmetric (entry (r, c) equals entry (c, r)); its eigenvalues lie within about -1.45 to 1.45. interval[0] lies in [-1.2, -0.7] and interval[1] in [1.45, 1.9].
All inputs are finite; a program needn't handle non-finite values.
Results may differ from a plain program's by a relative error of at most 0.0003.
Values sent between devices are 32-bit elements.
A program may use at most 128 MiB of HBM per device.

v0:
```python
import jax
import jax.numpy as jnp
from jax import lax
from jax.sharding import PartitionSpec as P

FILTER_DEG = 3
OUTER = 2


def scattered(contribution, width, axis):
    whole = contribution(jnp.int32(0), width * lax.axis_size(axis))
    return lax.psum_scatter(whole, axis, scatter_dimension=0, tiled=True)


def spread(array, axis, root):
    mine = lax.axis_index(axis) == root
    return lax.psum(jnp.where(mine, array, jnp.zeros_like(array)), axis)


def product(left, right):
    return jnp.dot(left, right, precision=lax.Precision.HIGHEST, preferred_element_type=jnp.float32)


def tri_solve(factor, values):
    return jax.scipy.linalg.solve_triangular(factor, values, lower=True)


def on_device(matrix, start_vectors, interval):
    block_rows, block_cols = matrix.shape
    slab_rows = start_vectors.shape[0]
    total_rows = slab_rows * lax.axis_size("row") * lax.axis_size("col")
    row_index = lax.axis_index("row")
    col_index = lax.axis_index("col")
    center = 0.5 * (interval[0] + interval[1])
    half_width = 0.5 * (interval[1] - interval[0])
    global_rows = row_index * block_rows + lax.iota(jnp.int32, block_rows)
    global_cols = col_index * block_cols + lax.iota(jnp.int32, block_cols)
    diagonal = global_rows[:, None] == global_cols[None, :]
    shifted = jnp.where(diagonal, matrix - center, matrix) / half_width

    def forward(col_full):

        def term(first_row, row_count):
            strip = lax.dynamic_slice_in_dim(shifted, first_row, row_count, 0)
            return product(strip, col_full)

        return scattered(term, slab_rows, "col")

    def gather_rows(slab_part):
        return lax.all_gather(slab_part, "col", axis=0, tiled=True)

    def to_columns(row_full):
        root_row = col_index * block_cols // block_rows
        offset = col_index * block_cols - root_row * block_rows
        column_part = lax.dynamic_slice_in_dim(row_full, offset, block_cols, 0)
        return spread(column_part, "row", root_row)

    def backward(row_full):
        partial_value = lax.dot_general(
            shifted,
            row_full,
            (((0,), (0,)), ((), ())),
            precision=lax.Precision.HIGHEST,
            preferred_element_type=jnp.float32,
        )
        return lax.psum(partial_value, "row")

    current_start = lax.all_gather(start_vectors, "row", axis=0, tiled=True)
    for sweep_index in range(OUTER):
        even_cols = current_start
        odd_slab = forward(current_start)
        odd_rows = gather_rows(odd_slab)
        for degree in range(2, FILTER_DEG + 1):
            if degree % 2 == 0:
                even_cols = 2.0 * backward(odd_rows) - even_cols
            else:
                odd_slab = 2.0 * forward(even_cols) - odd_slab
                odd_rows = gather_rows(odd_slab)
        final_cols = to_columns(odd_rows)
        mapped_cols = backward(odd_rows)
        final_slab = lax.dynamic_slice_in_dim(final_cols, row_index * slab_rows, slab_rows, 0)
        mapped_slab = lax.dynamic_slice_in_dim(mapped_cols, row_index * slab_rows, slab_rows, 0)
        gram_part = product(final_slab.T, final_slab)
        cross_part = product(final_slab.T, mapped_slab)
        gram_total = lax.psum(gram_part, ("row", "col"))
        cross_total = lax.psum(cross_part, ("row", "col"))
        gram_matrix = gram_total / total_rows
        cross_terms = cross_total / total_rows
        factor = jnp.linalg.cholesky(gram_matrix)
        basis_cols = tri_solve(factor, final_cols.T).T
        partial_proj = tri_solve(factor, cross_terms)
        projected = tri_solve(factor, partial_proj.T).T
        current_start = basis_cols
    basis_slab = lax.dynamic_slice_in_dim(current_start, row_index * slab_rows, slab_rows, 0)
    residual = tri_solve(factor, mapped_slab.T).T - product(basis_slab, projected)
    return (basis_slab, projected, residual)


def solution(mesh):
    return jax.shard_map(
        on_device,
        mesh=mesh,
        in_specs=(P("row", "col"), P(("col", "row"), None), P()),
        out_specs=(P(("col", "row"), None), P(), P(("col", "row"), None)),
        check_vma=False,
    )
```

profile of v0, /device:TPU:0, one launch (start us, length us, event | category | flops | bytes accessed | tf_op | source)
XLA Modules:
  0.0 1179.7 jit_solution(1612085924572650123)
XLA Ops:
  11.0 8.9 all_gather.15
  22.0 65.1 %reduce-scatter.5.cloned.1.call-done = f32[64,512]{1,0:T(8,128)} async-done(((f32[512,512]{1,0:T(8,128)}), f32[64,512]{1,0:T(8,128)}) %reduce-scatter.5.cloned.1.call-update) | async-done | bytes 131088 | tf_op jit(solution)/shard_map/reduce_scatter | solution.py:12
  87.2 41.3 %all-gather.5.cloned.1.call-done = f32[512,512]{1,0:T(8,128)} async-done(((f32[64,512]{1,0:T(8,128)}), f32[512,512]{1,0:T(8,128)}) %all-gather.5.cloned.1.call-update) | async-done | bytes 1048592 | tf_op jit(solution)/shard_map/all_gather | solution.py:50
  132.7 32.0 %all-reduce.10.cloned.1.call-done = f32[256,512]{0,1:T(8,128)} async-done(((f32[256,512]{0,1:T(8,128)}), f32[256,512]{0,1:T(8,128)}) %all-reduce.10.cloned.1.call-update) | async-done | bytes 524304 | tf_op jit(solution)/shard_map/psum | solution.py:66
  167.9 65.6 %reduce-scatter.7.cloned.1.call-done = f32[64,512]{1,0:T(8,128)} async-done(((f32[512,512]{1,0:T(8,128)}), f32[64,512]{1,0:T(8,128)}) %reduce-scatter.7.cloned.1.call-update) | async-done | bytes 131088 | tf_op jit(solution)/shard_map/reduce_scatter | solution.py:12
  235.3 40.1 %all-gather.7.cloned.1.call-done = f32[512,512]{1,0:T(8,128)} async-done(((f32[64,512]{1,0:T(8,128)}), f32[512,512]{1,0:T(8,128)}) %all-gather.7.cloned.1.call-update) | async-done | bytes 1048592 | tf_op jit(solution)/shard_map/all_gather | solution.py:50
  277.3 33.0 %all-reduce.12.cloned.1.call-done = f32[256,512]{1,0:T(8,128)} async-done(((f32[256,512]{1,0:T(8,128)}), f32[256,512]{1,0:T(8,128)}) %all-reduce.12.cloned.1.call-update) | async-done | bytes 524304 | tf_op jit(solution)/shard_map/psum | solution.py:17
  313.5 133.4 %all-reduce.14.cloned.1.call-done = f32[512,512]{0,1:T(8,128)} async-done(((f32[512,512]{0,1:T(8,128)}), f32[512,512]{0,1:T(8,128)}) %all-reduce.14.cloned.1.call-update) | async-done | bytes 1048592 | tf_op jit(solution)/shard_map/psum | solution.py:85
  449.7 11.7 cholesky.286
  461.5 9.8 custom-call.36
  472.1 11.7 cholesky.305
  483.8 10.0 custom-call.37
  494.5 11.7 cholesky.326
  507.0 9.8 custom-call.38
  517.4 11.7 cholesky.343
  533.6 8.5 while.9
  542.1 39.3 %custom-call.39 = f32[4,128,128]{1,2,0:T(8,128)S(1)} custom-call(f32[4,128,128]{2,1,0:T(8,128)S(1)} %get-tuple-element.42), custom_call_target="InvertDiagBlocksLowerTriangular" | custom-call | tf_op jit(solution)/shard_map/jit(_solve_triangular)/triangular_solve | solution.py:25
  586.6 63.4 %reduce-scatter.9.cloned.1.call-done = f32[64,512]{1,0:T(8,128)} async-done(((f32[512,512]{1,0:T(8,128)}), f32[64,512]{1,0:T(8,128)}) %reduce-scatter.9.cloned.1.call-update) | async-done | bytes 131088 | tf_op jit(solution)/shard_map/reduce_scatter | solution.py:12
  650.1 41.3 %all-gather.9.cloned.1.call-done = f32[512,512]{1,0:T(8,128)} async-done(((f32[64,512]{1,0:T(8,128)}), f32[512,512]{1,0:T(8,128)}) %all-gather.9.cloned.1.call-update) | async-done | bytes 1048592 | tf_op jit(solution)/shard_map/all_gather | solution.py:50
  695.4 32.2 %all-reduce.16.cloned.1.call-done = f32[256,512]{0,1:T(8,128)} async-done(((f32[256,512]{0,1:T(8,128)}), f32[256,512]{0,1:T(8,128)}) %all-reduce.16.cloned.1.call-update) | async-done | bytes 524304 | tf_op jit(solution)/shard_map/psum | solution.py:66
  730.8 65.8 %reduce-scatter.11.cloned.1.call-done = f32[64,512]{1,0:T(8,128)} async-done(((f32[512,512]{1,0:T(8,128)}), f32[64,512]{1,0:T(8,128)}) %reduce-scatter.11.cloned.1.call-update) | async-done | bytes 131088 | tf_op jit(solution)/shard_map/reduce_scatter | solution.py:12
  798.2 40.2 %all-gather.11.cloned.1.call-done = f32[512,512]{1,0:T(8,128)} async-done(((f32[64,512]{1,0:T(8,128)}), f32[512,512]{1,0:T(8,128)}) %all-gather.11.cloned.1.call-update) | async-done | bytes 1048592 | tf_op jit(solution)/shard_map/all_gather | solution.py:50
  842.8 35.0 %all-reduce.20.cloned.1.call-done = (f32[256,512]{1,0:T(8,128)}, f32[256,512]{1,0:T(8,128)}) async-done(((f32[256,512]{1,0:T(8,128)}, f32[256,512]{1,0:T(8,128)}), (f32[256,512]{1,0:T(8,128)}, f32[256,512]{1,0:T(8,128)})) %all-reduce.20.cloned.1.call-update) | async-done | bytes 1048592 | tf_op jit(solution)/shard_map/psum | solution.py:17
  883.7 135.3 %all-reduce.18.cloned.1.call-done = (f32[512,512]{0,1:T(8,128)}, f32[512,512]{0,1:T(8,128)}) async-done(((f32[512,512]{0,1:T(8,128)}, f32[512,512]{0,1:T(8,128)}), (f32[512,512]{0,1:T(8,128)}, f32[512,512]{0,1:T(8,128)})) %all-reduce.18.cloned.1.call-update) | async-done | bytes 2097168 | tf_op jit(solution)/shard_map/psum | solution.py:85
  1022.1 11.7 cholesky.358
  1034.5 9.8 custom-call.40
  1045.1 12.1 %cholesky.377 = f32[128,128]{1,0:T(8,128)S(1)} custom-call(f32[128,128]{1,0:T(8,128)S(1)} %cholesky.443), custom_call_target="Cholesky" | custom-call | tf_op jit(solution)/shard_map/jit(cholesky)/cholesky | solution.py:89
  1057.9 9.8 custom-call.41
  1068.4 11.7 cholesky.398
  1080.8 9.8 custom-call.42
  1091.2 11.7 cholesky.415
  1114.8 39.5 %custom-call.43 = f32[4,128,128]{1,2,0:T(8,128)S(1)} custom-call(f32[4,128,128]{2,1,0:T(8,128)S(1)} %get-tuple-element.43), custom_call_target="InvertDiagBlocksLowerTriangular" | custom-call | tf_op jit(solution)/shard_map/jit(_solve_triangular)/triangular_solve | solution.py:25
  (185 shorter events, 101.1 us)
Async XLA Ops:
  7.2 0.7 copy-start.9
  7.2 12.7 %copy-start.10 = (f32[512,256]{1,0:T(8,128)S(1)}, f32[512,256]{1,0:T(8,128)}, u32[]{:S(2)}) copy-start(f32[512,256]{1,0:T(8,128)} %param.8) | copy-start | bytes 1572868
  7.2 80.0 %reduce-scatter.5.cloned.1.call-start = ((), (), s32[]{:S(2)}) async-start(), calls=%async_computation.4 | async-start | bytes 1179648 | tf_op jit(solution)/shard_map/reduce_scatter | solution.py:12
  22.0 106.6 %all-gather.5.cloned.1.call-start = ((), (), s32[]{:S(2)}) async-start(), calls=%async_computation.5 | async-start | bytes 1179648 | tf_op jit(solution)/shard_map/all_gather | solution.py:50
  87.2 77.6 %all-reduce.10.cloned.1.call-start = ((), (), s32[]{:S(2)}) async-start(), calls=%async_computation.6 | async-start | bytes 1048576 | tf_op jit(solution)/shard_map/psum | solution.py:66
  132.5 101.1 %reduce-scatter.7.cloned.1.call-start = ((), (), s32[]{:S(2)}) async-start(), calls=%async_computation.7 | async-start | bytes 1179648 | tf_op jit(solution)/shard_map/reduce_scatter | solution.py:12
  167.9 65.7 %copy-start.6 = (f32[64,512]{1,0:T(8,128)S(1)}, f32[64,512]{1,0:T(8,128)}, u32[]{:S(2)}) copy-start(f32[64,512]{1,0:T(8,128)} %reduce-scatter.5.cloned.1.call-done) | copy-start | bytes 393220
  167.9 107.5 %all-gather.7.cloned.1.call-start = ((), (), s32[]{:S(2)}) async-start(), calls=%async_computation.8 | async-start | bytes 1179648 | tf_op jit(solution)/shard_map/all_gather | solution.py:50
  235.2 75.1 %all-reduce.12.cloned.1.call-start = ((), (), s32[]{:S(2)}) async-start(), calls=%async_computation.9 | async-start | bytes 1048576 | tf_op jit(solution)/shard_map/psum | solution.py:17
  277.3 169.7 %all-reduce.14.cloned.1.call-start = ((), (), s32[]{:S(2)}) async-start(), calls=%async_computation.10 | async-start | bytes 2097152 | tf_op jit(solution)/shard_map/psum | solution.py:85
  313.3 336.7 %reduce-scatter.9.cloned.1.call-start = ((), (), s32[]{:S(2)}) async-start(), calls=%async_computation.11 | async-start | bytes 1179648 | tf_op jit(solution)/shard_map/reduce_scatter | solution.py:12
  448.3 1.2 copy-start.1
  533.4 48.0 %copy-start.4 = (f32[256,512]{1,0:T(8,128)S(1)}, f32[256,512]{1,0:T(8,128)}, u32[]{:S(2)}) copy-start(f32[256,512]{1,0:T(8,128)} %all-reduce.12.cloned.1.call-done) | copy-start | bytes 1572868
  583.3 1.2 copy-start.11
  586.6 104.8 %all-gather.9.cloned.1.call-start = ((), (), s32[]{:S(2)}) async-start(), calls=%async_computation.12 | async-start | bytes 1179648 | tf_op jit(solution)/shard_map/all_gather | solution.py:50
  650.0 77.6 %all-reduce.16.cloned.1.call-start = ((), (), s32[]{:S(2)}) async-start(), calls=%async_computation.13 | async-start | bytes 1048576 | tf_op jit(solution)/shard_map/psum | solution.py:66
  695.3 101.2 %reduce-scatter.11.cloned.1.call-start = ((), (), s32[]{:S(2)}) async-start(), calls=%async_computation.14 | async-start | bytes 1179648 | tf_op jit(solution)/shard_map/reduce_scatter | solution.py:12
  730.7 65.8 %copy-start.5 = (f32[64,512]{1,0:T(8,128)S(1)}, f32[64,512]{1,0:T(8,128)}, u32[]{:S(2)}) copy-start(f32[64,512]{1,0:T(8,128)} %reduce-scatter.9.cloned.1.call-done) | copy-start | bytes 393220
  730.7 107.6 %all-gather.11.cloned.1.call-start = ((), (), s32[]{:S(2)}) async-start(), calls=%async_computation.15 | async-start | bytes 1179648 | tf_op jit(solution)/shard_map/all_gather | solution.py:50
  798.2 79.6 %all-reduce.20.cloned.1.call-start = ((), (), s32[]{:S(2)}) async-start(), calls=%async_computation.17 | async-start | bytes 2097152 | tf_op jit(solution)/shard_map/psum | solution.py:17
  838.4 3.3 copy-start.7
  842.6 176.4 %all-reduce.18.cloned.1.call-start = ((), (), s32[]{:S(2)}) async-start(), calls=%async_computation.16 | async-start | bytes 4194304 | tf_op jit(solution)/shard_map/psum | solution.py:85
  877.8 3.0 copy-start.8
  1019.0 2.4 copy-start
  1154.7 1.3 copy-start.3
  1158.0 2.1 copy-start.2
Sparse Core Ops, SparseCore 0:
  22.1 65.0 reduce-scatter.4
  89.3 39.2 all-gather.4
  132.6 32.0 all-reduce.9
  168.6 64.9 reduce-scatter.6
  236.1 39.1 all-gather.6
  278.2 32.0 all-reduce.11
  316.1 130.8 all-reduce.13
  586.7 63.2 reduce-scatter.8
  652.1 39.2 all-gather.8
  695.4 32.1 all-reduce.15
  731.6 64.9 reduce-scatter.10
  799.1 39.2 all-gather.10
  842.7 35.0 all-reduce.19
  883.8 135.1 all-reduce.17
where the time goes:
time: 1190 us; the launch traced here: 1180 us
  waiting for transfers between devices  824 us (69%)
  other arithmetic  248 us (21%)
  matrix products  53.3 us (4%)
  between operations  22.6 us (2%)
  local copies, waits for them, and re-layouts  22.2 us (2%)
    psum x2, waiting for transfers between devices, on_device(): gram_total = lax.psum(gram_part, ('row', 'col'))  269 us
    reduce_scatter x4, waiting for transfers between devices, scattered(): return lax.psum_scatter(whole, axis, scatter_dimension=0, tiled=True)  260 us
    all_gather x4, waiting for transfers between devices, gather_rows(): return lax.all_gather(slab_part, 'col', axis=0, tiled=True)  163 us
    another operation x29, other arithmetic, on_device(): factor = jnp.linalg.cholesky(gram_matrix)  158 us
    another operation x6, other arithmetic, tri_solve(): return jax.scipy.linalg.solve_triangular(factor, values, lower=True)  79.2 us
    psum x2, waiting for transfers between devices, spread(): return lax.psum(jnp.where(mine, array, jnp.zeros_like(array)), axis)  67.9 us
    psum x2, waiting for transfers between devices, backward(): return lax.psum(partial_value, 'row')  64.2 us
  transfers between devices with their start and end apart: 14, of which 14 were waited for; matrix products, arithmetic and copies ran while one was open for 0% of the time, Pallas kernels for 0%

commit v1 on v0

--- a/solution.py
+++ b/solution.py
@@ -82,7 +82,7 @@
         mapped_slab = lax.dynamic_slice_in_dim(mapped_cols, row_index * slab_rows, slab_rows, 0)
         gram_part = product(final_slab.T, final_slab)
         cross_part = product(final_slab.T, mapped_slab)
-        gram_total = lax.psum(gram_part, ("row", "col"))
+        gram_total = jnp.sum(lax.all_gather(gram_part, ("row", "col")), axis=0)
         cross_total = lax.psum(cross_part, ("row", "col"))
         gram_matrix = gram_total / total_rows
         cross_terms = cross_total / total_rows

time: 1190 us -> 1470 us (1.24)
  waiting for transfers between devices: 824 us -> 1070 us
  other arithmetic: 248 us -> 273 us
    all_gather x0 -> x2, waiting for transfers between devices: none -> 389 us  [on_device(): gram_total = jnp.sum(lax.all_gather(gram_part, ('row', 'col')), axis=0)]
    psum x2 -> x1, waiting for transfers between devices: 269 us -> 129 us  [on_device(): cross_total = lax.psum(cross_part, ('row', 'col'))]
    reduce_sum x0 -> x2, other arithmetic: none -> 25.1 us  [on_device(): gram_total = jnp.sum(lax.all_gather(gram_part, ('row', 'col')), axis=0)]
  transfers between devices with their start and end apart: 14 -> 15, of which waited for: 14 -> 15; matrix products, arithmetic and copies ran while one was open for 0% -> 0% of each run, Pallas kernels for 0% -> 0%
where the time goes in v1:
time: 1470 us
  waiting for transfers between devices  1070 us (73%)
  other arithmetic  273 us (19%)
  matrix products  67 us (5%)
  local copies, waits for them, and re-layouts  22.5 us (2%)
  between operations  22.5 us (2%)
    all_gather x2, waiting for transfers between devices, on_device(): gram_total = jnp.sum(lax.all_gather(gram_part, ('row', 'col')), axis=0)  389 us
    reduce_scatter x4, waiting for transfers between devices, scattered(): return lax.psum_scatter(whole, axis, scatter_dimension=0, tiled=True)  259 us
    all_gather x4, waiting for transfers between devices, gather_rows(): return lax.all_gather(slab_part, 'col', axis=0, tiled=True)  163 us
    another operation x29, other arithmetic, on_device(): factor = jnp.linalg.cholesky(gram_matrix)  158 us
    psum x1, waiting for transfers between devices, on_device(): cross_total = lax.psum(cross_part, ('row', 'col'))  129 us
    another operation x6, other arithmetic, tri_solve(): return jax.scipy.linalg.solve_triangular(factor, values, lower=True)  79.2 us
    psum x2, waiting for transfers between devices, spread(): return lax.psum(jnp.where(mine, array, jnp.zeros_like(array)), axis)  68.1 us
    psum x2, waiting for transfers between devices, backward(): return lax.psum(partial_value, 'row')  64.2 us
  transfers between devices with their start and end apart: 15, of which 15 were waited for; matrix products, arithmetic and copies ran while one was open for 0% of the time, Pallas kernels for 0%

profile of v1, /device:TPU:0, one launch (start us, length us, event | category | flops | bytes accessed | tf_op | source)
XLA Modules:
  0.0 1466.5 jit_solution(9582352364889395421)
XLA Ops:
  23.2 65.1 %reduce-scatter.5.cloned.1.call-done = f32[64,512]{1,0:T(8,128)} async-done(((f32[512,512]{1,0:T(8,128)}), f32[64,512]{1,0:T(8,128)}) %reduce-scatter.5.cloned.1.call-update) | async-done | bytes 131088 | tf_op jit(solution)/shard_map/reduce_scatter | solution.py:12
  88.4 41.3 %all-gather.9.cloned.1.call-done = f32[512,512]{1,0:T(8,128)} async-done(((f32[64,512]{1,0:T(8,128)}), f32[512,512]{1,0:T(8,128)}) %all-gather.9.cloned.1.call-update) | async-done | bytes 1048592 | tf_op jit(solution)/shard_map/all_gather | solution.py:50
  134.0 32.0 %all-reduce.8.cloned.1.call-done = f32[256,512]{0,1:T(8,128)} async-done(((f32[256,512]{0,1:T(8,128)}), f32[256,512]{0,1:T(8,128)}) %all-reduce.8.cloned.1.call-update) | async-done | bytes 524304 | tf_op jit(solution)/shard_map/psum | solution.py:66
  169.4 65.5 %reduce-scatter.7.cloned.1.call-done = f32[64,512]{1,0:T(8,128)} async-done(((f32[512,512]{1,0:T(8,128)}), f32[64,512]{1,0:T(8,128)}) %reduce-scatter.7.cloned.1.call-update) | async-done | bytes 131088 | tf_op jit(solution)/shard_map/reduce_scatter | solution.py:12
  236.6 40.1 %all-gather.11.cloned.1.call-done = f32[512,512]{1,0:T(8,128)} async-done(((f32[64,512]{1,0:T(8,128)}), f32[512,512]{1,0:T(8,128)}) %all-gather.11.cloned.1.call-update) | async-done | bytes 1048592 | tf_op jit(solution)/shard_map/all_gather | solution.py:50
  278.6 33.0 %all-reduce.10.cloned.1.call-done = f32[256,512]{1,0:T(8,128)} async-done(((f32[256,512]{1,0:T(8,128)}), f32[256,512]{1,0:T(8,128)}) %all-reduce.10.cloned.1.call-update) | async-done | bytes 524304 | tf_op jit(solution)/shard_map/psum | solution.py:17
  314.7 194.8 %all-gather.17.cloned.1.call-done = f32[16384,512]{1,0:T(8,128)} async-done(((f32[512,512]{1,0:T(8,128)}), f32[16384,512]{1,0:T(8,128)}) %all-gather.17.cloned.1.call-update) | async-done | bytes 33554448 | tf_op jit(solution)/shard_map/all_gather | solution.py:85
  509.5 12.4 reduce_sum.18
  523.0 11.7 cholesky.286
  534.8 9.8 custom-call.36
  545.3 11.7 cholesky.305
  557.1 10.2 custom-call.37
  567.9 11.7 cholesky.326
  590.8 11.9 cholesky.343
  615.2 39.3 %custom-call.39 = f32[4,128,128]{1,2,0:T(8,128)S(1)} custom-call(f32[4,128,128]{2,1,0:T(8,128)S(1)} %get-tuple-element.42), custom_call_target="InvertDiagBlocksLowerTriangular" | custom-call | tf_op jit(solution)/shard_map/jit(_solve_triangular)/triangular_solve | solution.py:25
  664.4 62.4 %reduce-scatter.9.cloned.1.call-done = f32[64,512]{1,0:T(8,128)} async-done(((f32[512,512]{1,0:T(8,128)}), f32[64,512]{1,0:T(8,128)}) %reduce-scatter.9.cloned.1.call-update) | async-done | bytes 131088 | tf_op jit(solution)/shard_map/reduce_scatter | solution.py:12
  726.9 41.3 %all-gather.13.cloned.1.call-done = f32[512,512]{1,0:T(8,128)} async-done(((f32[64,512]{1,0:T(8,128)}), f32[512,512]{1,0:T(8,128)}) %all-gather.13.cloned.1.call-update) | async-done | bytes 1048592 | tf_op jit(solution)/shard_map/all_gather | solution.py:50
  772.4 32.2 %all-reduce.12.cloned.1.call-done = f32[256,512]{0,1:T(8,128)} async-done(((f32[256,512]{0,1:T(8,128)}), f32[256,512]{0,1:T(8,128)}) %all-reduce.12.cloned.1.call-update) | async-done | bytes 524304 | tf_op jit(solution)/shard_map/psum | solution.py:66
  808.0 65.6 %reduce-scatter.11.cloned.1.call-done = f32[64,512]{1,0:T(8,128)} async-done(((f32[512,512]{1,0:T(8,128)}), f32[64,512]{1,0:T(8,128)}) %reduce-scatter.11.cloned.1.call-update) | async-done | bytes 131088 | tf_op jit(solution)/shard_map/reduce_scatter | solution.py:12
  875.3 40.1 %all-gather.15.cloned.1.call-done = f32[512,512]{1,0:T(8,128)} async-done(((f32[64,512]{1,0:T(8,128)}), f32[512,512]{1,0:T(8,128)}) %all-gather.15.cloned.1.call-update) | async-done | bytes 1048592 | tf_op jit(solution)/shard_map/all_gather | solution.py:50
  920.7 35.1 %all-reduce.16.cloned.1.call-done = (f32[256,512]{1,0:T(8,128)}, f32[256,512]{1,0:T(8,128)}) async-done(((f32[256,512]{1,0:T(8,128)}, f32[256,512]{1,0:T(8,128)}), (f32[256,512]{1,0:T(8,128)}, f32[256,512]{1,0:T(8,128)})) %all-reduce.16.cloned.1.call-update) | async-done | bytes 1048592 | tf_op jit(solution)/shard_map/psum | solution.py:17
  962.9 129.2 %all-reduce.14.cloned.1.call-done = f32[512,512]{0,1:T(8,128)} async-done(((f32[512,512]{0,1:T(8,128)}), f32[512,512]{0,1:T(8,128)}) %all-reduce.14.cloned.1.call-update) | async-done | bytes 1048592 | tf_op jit(solution)/shard_map/psum | solution.py:86
  1094.4 194.2 %all-gather.19.cloned.1.call-done = f32[16384,512]{1,0:T(8,128)} async-done(((f32[512,512]{1,0:T(8,128)}), f32[16384,512]{1,0:T(8,128)}) %all-gather.19.cloned.1.call-update) | async-done | bytes 33554448 | tf_op jit(solution)/shard_map/all_gather | solution.py:85
  1288.6 12.7 reduce_sum.19
  1302.4 11.7 cholesky.358
  1314.2 9.8 custom-call.40
  1324.7 11.7 cholesky.377
  1337.7 9.9 custom-call.41
  1348.4 11.7 cholesky.398
  1360.8 9.8 custom-call.42
  1371.2 11.7 cholesky.415
  1394.3 39.5 %custom-call.43 = f32[4,128,128]{1,2,0:T(8,128)S(1)} custom-call(f32[4,128,128]{2,1,0:T(8,128)S(1)} %get-tuple-element.43), custom_call_target="InvertDiagBlocksLowerTriangular" | custom-call | tf_op jit(solution)/shard_map/jit(_solve_triangular)/triangular_solve | solution.py:25
  (168 shorter events, 140.9 us)
Async XLA Ops:
  7.2 81.1 %reduce-scatter.5.cloned.1.call-start = ((), (), s32[]{:S(2)}) async-start(), calls=%async_computation.4 | async-start | bytes 1179648 | tf_op jit(solution)/shard_map/reduce_scatter | solution.py:12
  23.1 106.5 %all-gather.9.cloned.1.call-start = ((), (), s32[]{:S(2)}) async-start(), calls=%async_computation.5 | async-start | bytes 1179648 | tf_op jit(solution)/shard_map/all_gather | solution.py:50
  88.3 77.7 %all-reduce.8.cloned.1.call-start = ((), (), s32[]{:S(2)}) async-start(), calls=%async_computation.6 | async-start | bytes 1048576 | tf_op jit(solution)/shard_map/psum | solution.py:66
  133.8 101.1 %reduce-scatter.7.cloned.1.call-start = ((), (), s32[]{:S(2)}) async-start(), calls=%async_computation.7 | async-start | bytes 1179648 | tf_op jit(solution)/shard_map/reduce_scatter | solution.py:12
  169.3 107.3 %all-gather.11.cloned.1.call-start = ((), (), s32[]{:S(2)}) async-start(), calls=%async_computation.8 | async-start | bytes 1179648 | tf_op jit(solution)/shard_map/all_gather | solution.py:50
  236.6 75.0 %all-reduce.10.cloned.1.call-start = ((), (), s32[]{:S(2)}) async-start(), calls=%async_computation.9 | async-start | bytes 1048576 | tf_op jit(solution)/shard_map/psum | solution.py:17
  278.6 230.9 %all-gather.17.cloned.1.call-start = ((), (), s32[]{:S(2)}) async-start(), calls=%async_computation.16 | async-start | bytes 34603008 | tf_op jit(solution)/shard_map/all_gather | solution.py:85
  314.6 412.2 %reduce-scatter.9.cloned.1.call-start = ((), (), s32[]{:S(2)}) async-start(), calls=%async_computation.10 | async-start | bytes 1179648 | tf_op jit(solution)/shard_map/reduce_scatter | solution.py:12
  664.4 103.9 %all-gather.13.cloned.1.call-start = ((), (), s32[]{:S(2)}) async-start(), calls=%async_computation.11 | async-start | bytes 1179648 | tf_op jit(solution)/shard_map/all_gather | solution.py:50
  726.9 77.7 %all-reduce.12.cloned.1.call-start = ((), (), s32[]{:S(2)}) async-start(), calls=%async_computation.12 | async-start | bytes 1048576 | tf_op jit(solution)/shard_map/psum | solution.py:66
  772.3 101.2 %reduce-scatter.11.cloned.1.call-start = ((), (), s32[]{:S(2)}) async-start(), calls=%async_computation.13 | async-start | bytes 1179648 | tf_op jit(solution)/shard_map/reduce_scatter | solution.py:12
  807.9 107.5 %all-gather.15.cloned.1.call-start = ((), (), s32[]{:S(2)}) async-start(), calls=%async_computation.14 | async-start | bytes 1179648 | tf_op jit(solution)/shard_map/all_gather | solution.py:50
  875.2 80.7 %all-reduce.16.cloned.1.call-start = ((), (), s32[]{:S(2)}) async-start(), calls=%async_computation.18 | async-start | bytes 2097152 | tf_op jit(solution)/shard_map/psum | solution.py:17
  920.7 171.4 %all-reduce.14.cloned.1.call-start = ((), (), s32[]{:S(2)}) async-start(), calls=%async_computation.15 | async-start | bytes 2097152 | tf_op jit(solution)/shard_map/psum | solution.py:86
  958.9 329.8 %all-gather.19.cloned.1.call-start = ((), (), s32[]{:S(2)}) async-start(), calls=%async_computation.17 | async-start | bytes 34603008 | tf_op jit(solution)/shard_map/all_gather | solution.py:85
Sparse Core Ops, SparseCore 0:
  23.3 65.0 reduce-scatter.4
  90.4 39.1 all-gather.8
  133.9 32.0 all-reduce.7
  169.9 64.9 reduce-scatter.6
  237.4 39.1 all-gather.10
  279.4 32.0 all-reduce.9
  315.1 194.2 all-gather.16
  664.5 62.3 reduce-scatter.8
  729.0 39.2 all-gather.12
  772.5 32.0 all-reduce.11
  808.6 64.9 reduce-scatter.10
  876.1 39.2 all-gather.14
  920.8 35.0 all-reduce.15
  960.9 131.1 all-reduce.13
  1095.5 193.1 all-gather.18
